TPU v7x, 32 devices: a whole 2x2x4 slice. The times are simulated.
32 devices in a mesh: grp: 2 (over x), seq: 8 (over z, y), head: 2 (over core).
Axes of the slice: x: 2, y: 2, z: 4, core: 2. Of those that a mesh axis runs over, the one named last changes fastest.
Arguments:
- features: bfloat16 [2, 8, 4, 32, 512], P('grp', 'seq', 'head'), may hold values from -6 to 6
- conv_weight: bfloat16 [3, 3, 3, 512, 16], replicated, may hold values from -0.0546875 to 0.0546875
- conv_bias: float32 [16], replicated, may hold values from -3 to 3
- token_order: int32 [256], P('seq'), may hold values from 0 to 255, each once
- embed_weight: bfloat16 [64, 3072], replicated, may hold values from -0.75 to 0.75
- norm_gain: float32 [3072], replicated, may hold values from 0.1 to 1.9
- qkv_weight: bfloat16 [3072, 3, 2048], P('seq', None, 'head'), may hold values from -0.109375 to 0.109375
- grad_out: bfloat16 [2, 256, 2048], P('grp', 'seq', 'head'), may hold values from -6 to 6
Outputs:
- attended: bfloat16 [2, 256, 2048], P('grp', 'seq', 'head')
- embed_grad: float32 [64, 3072], P(None, 'head')
All inputs are finite; a program needn't handle non-finite values.
Results may differ from a plain program's by a relative error of at most 0.0052.
Values may be sent and summed in bfloat16 or wider, within the bound.
A program may use at most 128 MiB of HBM per device.

v0:
```python
import functools

import jax
import jax.numpy as jnp
from jax import lax
from jax.experimental import pallas as pl
from jax.experimental.pallas import tpu as pltpu
from jax.sharding import PartitionSpec as P

D = 3072
HEAD_DIM = 64
MESH = pl.DeviceIdType.MESH


def shifted(value, axis, steps):
    count = lax.axis_size(axis)
    leading, last = (max(0, -steps), min(count, count - steps))
    return lax.ppermute(value, axis, [(source, source + steps) for source in range(leading, last)])


def extended(block, sides, width):
    for axis, dim in sides:
        count = lax.axis_size(axis)
        forward = [(i, i + 1) for i in range(count - 1)]
        backward = [(target, source) for source, target in forward]
        low = lax.ppermute(
            lax.slice_in_dim(block, block.shape[dim] - width, None, axis=dim), axis, forward
        )
        high = lax.ppermute(lax.slice_in_dim(block, 0, width, axis=dim), axis, backward)
        block = jnp.concatenate([low, block, high], axis=dim)
    return block


def patchify(latent):
    frames, rows, columns, channels = latent.shape
    blocks = latent.reshape(frames, rows // 2, 2, columns // 2, 2, channels)
    blocks = jnp.transpose(blocks, (0, 1, 3, 2, 4, 5))
    return blocks.reshape(frames * (rows // 2) * (columns // 2), 4 * channels)


def encode_tile(tile, conv_weight, conv_bias):
    frames, rows, columns, channels = tile.shape
    hops = (frames + 1) // frames
    earlier = []
    for hop in range(hops, 0, -1):
        earlier.append(shifted(tile, "seq", hop))
    stacked = jnp.concatenate(earlier + [tile], axis=0)
    padded = extended(stacked, (("head", 1),), 1)
    padded = jnp.pad(padded, ((0, 0), (0, 0), (1, 1), (0, 0)))
    total = jnp.zeros((frames * rows * columns, conv_weight.shape[-1]), jnp.float32) + conv_bias
    for a in range(3):
        for b in range(3):
            for e in range(3):
                piece = padded[a : a + frames, b : b + rows, e : e + columns].reshape(-1, channels)
                total = total + jnp.dot(
                    piece, conv_weight[a, b, e], preferred_element_type=jnp.float32
                )
    return total.astype(jnp.bfloat16).reshape(frames, rows, columns, conv_weight.shape[-1])


def head_major(matrix, head_local):
    count = matrix.shape[0]
    return jnp.transpose(matrix.reshape(count, head_local, HEAD_DIM), (1, 0, 2))


def row_major(stacked):
    heads_here, count, size = stacked.shape
    return jnp.transpose(stacked, (1, 0, 2)).reshape(count, heads_here * size)


def head_forward(operands):
    query, keys, values, cotan = operands
    factor = HEAD_DIM ** (-0.5)
    scores = jnp.dot(query, keys.T, preferred_element_type=jnp.float32) * factor
    top = jnp.max(scores, axis=-1, keepdims=True)
    lse = top + jnp.log(jnp.sum(jnp.exp(scores - top), axis=-1, keepdims=True))
    probs = jnp.exp(scores - lse)
    probs_low = probs.astype(jnp.bfloat16)
    output = jnp.dot(probs_low, values, preferred_element_type=jnp.float32).astype(jnp.bfloat16)
    delta = jnp.sum(cotan.astype(jnp.float32) * output.astype(jnp.float32), axis=-1, keepdims=True)
    dprob = jnp.dot(cotan, values.T, preferred_element_type=jnp.float32)
    dscore = (probs * (dprob - delta)).astype(jnp.bfloat16)
    grad_q = jnp.dot(dscore, keys, preferred_element_type=jnp.float32) * factor
    return (output, lse[:, 0], delta[:, 0], grad_q)


def head_backward(operands):
    query, cotan, lse_piece, delta_piece, own_keys, own_values = operands
    factor = HEAD_DIM ** (-0.5)
    scores = jnp.dot(query, own_keys.T, preferred_element_type=jnp.float32) * factor
    probs = jnp.exp(scores - lse_piece[:, None])
    value_add = jnp.dot(probs.astype(jnp.bfloat16).T, cotan, preferred_element_type=jnp.float32)
    dprob = jnp.dot(cotan, own_values.T, preferred_element_type=jnp.float32)
    dscore = (probs * (dprob - delta_piece[:, None])).astype(jnp.bfloat16)
    key_add = jnp.dot(dscore.T, query, preferred_element_type=jnp.float32)
    return (key_add, value_add)


def per_device(
    features, conv_weight, conv_bias, token_order, embed_weight, norm_gain, qkv_weight, grad_out
):
    tile = encode_tile(features[0], conv_weight, conv_bias)
    all_rows = lax.all_gather(tile, "head", axis=1, tiled=True)
    whole = lax.all_gather(all_rows, "seq", axis=0, tiled=True)
    patches = patchify(whole)
    tokens = jnp.take(patches, token_order, axis=0)
    local_rows = tokens.shape[0]
    mixed = jnp.dot(tokens, embed_weight, preferred_element_type=jnp.float32)
    inverse = lax.rsqrt(jnp.mean(mixed * mixed, axis=-1, keepdims=True) + 1e-06)
    normal = mixed * inverse
    hidden = (normal * norm_gain).astype(jnp.bfloat16)
    full_weight = lax.all_gather(qkv_weight, "seq", axis=0, tiled=True)
    local_width = full_weight.shape[2]
    head_local = local_width // HEAD_DIM
    flat_weight = full_weight.reshape(D, 3 * local_width)
    proj = jnp.dot(hidden, flat_weight, preferred_element_type=jnp.float32).astype(jnp.bfloat16)
    proj = proj.reshape(local_rows, 3, local_width)
    query = proj[:, 0]
    keys_all, values_all = (
        lax.all_gather(proj[:, 1], "seq", axis=0, tiled=True),
        lax.all_gather(proj[:, 2], "seq", axis=0, tiled=True),
    )
    cotan = grad_out[0]
    output_h, lse_h, delta_h, grad_q_h = lax.map(
        head_forward,
        (
            head_major(query, head_local),
            head_major(keys_all, head_local),
            head_major(values_all, head_local),
            head_major(cotan, head_local),
        ),
    )
    output = row_major(output_h)
    grad_q = row_major(grad_q_h)
    lse_all, delta_all = (
        lax.all_gather(jnp.transpose(lse_h), "seq", axis=0, tiled=True),
        lax.all_gather(jnp.transpose(delta_h), "seq", axis=0, tiled=True),
    )
    own_keys = head_major(proj[:, 1], head_local)
    own_values = head_major(proj[:, 2], head_local)
    query_piece = lax.all_gather(query, "seq", axis=0, tiled=True)
    cotan_piece = lax.all_gather(cotan, "seq", axis=0, tiled=True)
    lse_piece = jnp.transpose(lse_all)
    delta_piece = jnp.transpose(delta_all)
    key_add, value_add = lax.map(
        head_backward,
        (
            head_major(query_piece, head_local),
            head_major(cotan_piece, head_local),
            lse_piece,
            delta_piece,
            own_keys,
            own_values,
        ),
    )
    grad_k = row_major(key_add * HEAD_DIM ** (-0.5))
    grad_v = row_major(value_add)
    grads = (
        jnp.stack([grad_q, grad_k, grad_v], axis=1)
        .reshape(local_rows, 3 * local_width)
        .astype(jnp.bfloat16)
    )
    back_part = lax.dot_general(
        grads, flat_weight, (((1,), (1,)), ((), ())), preferred_element_type=jnp.float32
    )
    head_count_d = lax.axis_size("head")
    width_dev = D // head_count_d
    start_col = lax.axis_index("head") * width_dev
    normal_own = lax.dynamic_slice_in_dim(normal, start_col, width_dev, 1)
    gain_own = lax.dynamic_slice_in_dim(norm_gain, start_col, width_dev, 0)
    back_own = lax.psum_scatter(
        back_part.astype(jnp.bfloat16), "head", scatter_dimension=1, tiled=True
    ).astype(jnp.float32)
    scaled_own = back_own * gain_own
    inner_part = jnp.sum(scaled_own * normal_own, axis=-1, keepdims=True)
    inner = lax.psum(inner_part, "head") / D
    dmixed_own = inverse * (scaled_own - normal_own * inner)
    embed_part = jnp.dot(
        tokens.astype(jnp.float32).T,
        dmixed_own,
        preferred_element_type=jnp.float32,
        precision=lax.Precision.HIGHEST,
    )
    embed_grad = lax.psum(embed_part, ("grp", "seq"))
    attended = output.reshape(1, local_rows, local_width)
    return (attended, embed_grad)

def split2(value):
    high = value.astype(jnp.bfloat16)
    low = (value - high.astype(jnp.float32)).astype(jnp.bfloat16)
    return high, low


def mm(a, b, dims=((1,), (0,))):
    return lax.dot_general(a, b, (dims, ((), ())), preferred_element_type=jnp.float32)


NT = ((1,), (1,))
TN = ((0,), (0,))


def fused(
    groups, seq, feat_hbm, conv_hbm, bias_hbm, order_hbm, embed_hbm, gain_hbm, weight_hbm, cot_hbm,
    att_ref, grad_ref,
    feat_ref, conv_ref, bias_ref, order_ref, embed_ref, gain_ref, cot_ref,
    weight, mbuf, mrecv, cots, orders, halo_own, halo_par, halo_in, lat_acc, patches, att,
    gall, glast, part, rrecv, quarter, gathered,
    in_sem, w_sem, m_send, m_recv, c_send, c_recv, o_send, o_recv, h_send, h_recv, l_send, l_recv,
    t_send, t_recv, g_send, g_recv, b_send, b_recv, r_send, r_recv, f_send, f_recv, f_local,
):
    g, s, h = lax.axis_index("grp"), lax.axis_index("seq"), lax.axis_index("head")
    own_rows = cot_ref.shape[0]
    tokens_all = own_rows * seq
    depth = weight.shape[1]
    cols = att.shape[2]
    patch = embed_ref.shape[0]
    width_model = embed_ref.shape[1]
    lat_ch = bias_ref.shape[1]
    wide = 3 * cols
    far = lambda off: lax.rem(s + off, seq)

    barrier = pltpu.get_barrier_semaphore()
    for dg in range(groups):
        for ds in range(seq):
            for dh in range(2):
                if dg + ds + dh:
                    pl.semaphore_signal(
                        barrier, inc=1, device_id=(lax.rem(g + dg, groups), far(ds), lax.rem(h + dh, 2)),
                        device_id_type=MESH,
                    )
    w_copies = [pltpu.make_async_copy(weight_hbm.at[j], weight.at[j], w_sem.at[j]) for j in range(3)]
    in_copies = [
        pltpu.make_async_copy(src, dst, in_sem.at[i])
        for i, (src, dst) in enumerate(
            [
                (feat_hbm, feat_ref), (conv_hbm, conv_ref), (bias_hbm, bias_ref), (embed_hbm, embed_ref),
                (gain_hbm, gain_ref), (order_hbm, order_ref), (cot_hbm, cot_ref),
            ]
        )
    ]
    for c in in_copies + w_copies:
        c.start()
    in_copies[0].wait()
    in_copies[1].wait()

    def remote(src, dst, send, recv, to):
        return pltpu.make_async_remote_copy(
            src_ref=src, dst_ref=dst, send_sem=send, recv_sem=recv, device_id=to, device_id_type=MESH
        )

    block = feat_ref.shape[0] // 4
    ri = lax.broadcasted_iota(jnp.int32, (4 * block, 4 * block), 0)
    ci = lax.broadcasted_iota(jnp.int32, (4 * block, 4 * block), 1)
    src_row = (ri // (2 * block)) * (2 * block) + 2 * lax.rem(ri, block) + lax.rem(ri // block, 2)
    sel = jnp.where(ci == src_row, 1.0, 0.0).astype(jnp.bfloat16)
    feat = mm(sel, feat_ref[...]).astype(jnp.bfloat16)
    jrow = lax.broadcasted_iota(jnp.int32, (block, 1), 0)

    def down(x):
        return jnp.where(jrow == 0, 0.0, pltpu.roll(x, 1, 0))

    def up(x):
        return jnp.where(jrow == block - 1, 0.0, pltpu.roll(x, block - 1, 0))

    z = {}
    for b in range(3):
        y = []
        for e in range(3):
            w_be = jnp.concatenate(
                [conv_ref[((a * 3 + b) * 3 + e) * lat_ch : ((a * 3 + b) * 3 + e + 1) * lat_ch, :] for a in range(3)],
                axis=0,
            )
            out = mm(feat, w_be, NT)
            y.append([[out[(2 * r + q) * block : (2 * r + q + 1) * block] for q in range(2)] for r in range(2)])
        for r in range(2):
            z[b, r, 0] = y[1][r][0] + y[2][r][1] + down(y[0][r][1])
            z[b, r, 1] = y[1][r][1] + y[0][r][0] + up(y[2][r][0])
    own = [z[1, 0, q] + z[2, 1, q] for q in range(2)] + [z[0, 0, q] + z[1, 1, q] for q in range(2)]
    edge = [jnp.where(h == 0, z[0, 1, q], z[2, 0, q]) for q in range(2)]
    par = [jnp.where(h == 0, edge[q], 0.0) for q in range(2)] + [jnp.where(h == 0, 0.0, edge[q]) for q in range(2)]
    for a in range(3):
        lanes = slice(a * lat_ch, (a + 1) * lat_ch)
        halo_own[a] = jnp.concatenate([x[:, lanes] for x in own], axis=1)
        halo_par[a] = jnp.concatenate([x[:, lanes] for x in par], axis=1)

    for c in in_copies[2:]:
        c.wait()
    own_cols = pl.ds(pl.multiple_of(s * depth, 128), depth)
    embed_own = embed_ref[:, own_cols].astype(jnp.float32)
    gain_own = gain_ref[:, own_cols]
    eg_high, eg_low = split2(embed_own * gain_own)
    eg = jnp.concatenate([eg_high, eg_low], axis=0)

    pl.semaphore_wait(barrier, 2 * groups * seq - 1)

    hops = [(0, 1, halo_par, 2), (1, 0, halo_own, 1), (1, 1, halo_par, 1), (2, 0, halo_own, 0), (2, 1, halo_par, 0)]

    def halo_copy(i):
        ds, dh, src, a = hops[i]
        return remote(
            src.at[a], halo_in.at[i], h_send.at[i], h_recv.at[i], (g, lax.rem(s + ds, seq), lax.rem(h + dh, 2))
        )

    halo_copy(0).start()
    for i in range(1, 5):
        pl.when(s + hops[i][0] < seq)(lambda i=i: halo_copy(i).start())

    def order_copy(k):
        return remote(order_ref, orders.at[s], o_send.at[k - 1], o_recv.at[k - 1], (g, far(k), h))

    def cot_copy(k):
        return remote(
            cot_ref.at[:, pl.ds(pl.multiple_of(far(k) * cols, 128), cols)], cots.at[s],
            c_send.at[k - 1], c_recv.at[k - 1], (g, far(k), h),
        )

    for k in range(1, seq):
        order_copy(k).start()
    orders[s] = order_ref[...]
    cots[s] = cot_ref[:, pl.ds(pl.multiple_of(s * cols, 128), cols)]

    for j in range(3):
        w_copies[j].wait()
        prod = mm(eg, weight[j])
        prod = prod[:patch] + prod[patch:]
        for t in range(seq):
            mbuf[t, j] = prod[:, t * cols : (t + 1) * cols].astype(jnp.bfloat16)

    def m_copy(k):
        return remote(mbuf.at[far(k)], mrecv.at[k - 1], m_send.at[k - 1], m_recv.at[k - 1], (g, far(k), h))

    far_first = sorted(range(1, seq), key=lambda k: abs(k - seq // 2))
    for k in far_first[: seq // 2]:
        m_copy(k).start()

    halo_copy(0).wait_recv()
    lat_acc[...] = halo_own[2] + halo_in[0] + jnp.concatenate([bias_ref[...]] * 4, axis=1)
    for i in range(1, 5):

        def add(i=i):
            halo_copy(i).wait_recv()
            lat_acc[...] += halo_in[i]

        pl.when(s >= hops[i][0])(add)
    mine = 2 * s + h
    patches[mine] = lat_acc[...].astype(jnp.bfloat16)
    peers = [(ds, dh) for ds in range(seq) for dh in range(2) if ds + dh]

    def lat_copy(i):
        ds, dh = peers[i]
        return remote(
            patches.at[mine], patches.at[mine], l_send.at[i], l_recv.at[i], (g, far(ds), lax.rem(h + dh, 2))
        )

    for i in range(len(peers)):
        lat_copy(i).start()
    for k in far_first[seq // 2 :]:
        m_copy(k).start()
    for k in range(1, seq):
        cot_copy(k).start()

    for k in range(1, seq):
        order_copy(k).wait_recv()
    hot = jnp.concatenate(
        [
            jnp.where(
                lax.broadcasted_iota(jnp.int32, (tokens_all, own_rows), 0) == orders[t][:1], 1.0, 0.0
            )
            for t in range(seq)
        ],
        axis=1,
    ).astype(jnp.bfloat16)

    for i in range(len(peers)):
        lat_copy(i).wait_recv()
    tokens = mm(hot, patches[...].reshape(tokens_all, patch), TN).astype(jnp.bfloat16)
    square = jnp.zeros((tokens_all, 1), jnp.float32)
    chunk = depth
    for t in range(width_model // chunk):
        mixed = mm(tokens, embed_ref[:, t * chunk : (t + 1) * chunk])
        square = square + jnp.sum(mixed * mixed, axis=-1, keepdims=True)
    inverse = lax.rsqrt(square / width_model + 1e-06)

    total = [mbuf[s, j].astype(jnp.float32) for j in range(3)]
    for k in range(1, seq):
        m_copy(k).wait_recv()
        total = [total[j] + mrecv[k - 1, j].astype(jnp.float32) for j in range(3)]
    m_high, m_low = split2(jnp.concatenate(total, axis=1))
    proj = (mm(tokens, m_high) + mm(tokens, m_low)) * inverse
    low = proj.astype(jnp.bfloat16)

    for k in range(1, seq):
        cot_copy(k).wait_recv()
    cot_all = cots[...].reshape(tokens_all, cols)
    factor = HEAD_DIM ** (-0.5)
    half_patch = patch // 2
    scaled_tokens = tokens.astype(jnp.float32) * (inverse * inverse / width_model)
    outs = []
    inner = jnp.zeros((tokens_all, 1), jnp.float32)

    beside = s + 1 - 2 * lax.rem(s, 2)

    def g_copy(k, n):
        blocks, send, recv = (gall, g_send, g_recv) if n == 0 else (glast, b_send, b_recv)
        hop = seq // 2
        if k < hop:
            source, to = s, far(2 * k)
        elif k == hop:
            source, to = s, beside
        else:
            source, to = far(seq - 2 * (k - hop)), beside
        return remote(blocks.at[source], blocks.at[source], send.at[k - 1], recv.at[k - 1], (g, to, h))

    for n in range(2):
        lanes = lambda j: slice(j * cols + n * HEAD_DIM, j * cols + (n + 1) * HEAD_DIM)
        query, keys, values = low[:, lanes(0)], low[:, lanes(1)], low[:, lanes(2)]
        cotan = cot_all[:, lanes(0)]
        scores = mm(query, keys, NT) * factor
        top = jnp.max(scores, axis=-1, keepdims=True)
        expd = jnp.exp(scores - top)
        probs = expd * (1.0 / jnp.sum(expd, axis=-1, keepdims=True))
        probs_low = probs.astype(jnp.bfloat16)
        output = mm(probs_low, values).astype(jnp.bfloat16)
        delta = jnp.sum(cotan.astype(jnp.float32) * output.astype(jnp.float32), axis=-1, keepdims=True)
        dprob = mm(cotan, values, NT)
        dscore = (probs * (dprob - delta)).astype(jnp.bfloat16)
        outs.append(output)
        parts = [mm(dscore, keys) * factor, mm(dscore, query, TN) * factor, mm(probs_low, cotan, TN)]
        parts = [x.astype(jnp.bfloat16).astype(jnp.float32) for x in parts]
        for j in range(3):
            inner = inner + jnp.sum(parts[j] * proj[:, lanes(j)], axis=-1, keepdims=True)
        rhs = [x * inverse for x in parts]
        if n == 1:
            rhs.append(scaled_tokens * inner)
        rhs_high, rhs_low = split2(jnp.concatenate(rhs, axis=1))
        made = mm(tokens, rhs_high, TN) + mm(tokens, rhs_low, TN)
        packed = [made[:, : 2 * HEAD_DIM]]
        for j in range(2, len(rhs)):
            piece = made[:, j * HEAD_DIM : (j + 1) * HEAD_DIM]
            packed.append(jnp.concatenate([piece[:half_patch], piece[half_patch:]], axis=1))
        (gall if n == 0 else glast)[s] = jnp.concatenate(packed, axis=0).astype(jnp.bfloat16)
        for k in range(1, seq // 2 + 1):
            g_copy(k, n).start()
    att[...] = jnp.concatenate(outs, axis=1).reshape(seq, own_rows, cols)
    here = pl.ds(pl.multiple_of(s * cols, 128), cols)

    def att_copy(k):
        return remote(att.at[far(k)], att_ref.at[:, here], t_send.at[k - 1], t_recv.at[k - 1], (g, far(k), h))

    att_ref[:, here] = att[s]

    for n in range(2):
        for k in range(1, seq // 2):
            g_copy(k, n).wait_recv()
            g_copy(seq // 2 + k, n).start()
    for k in range(1, seq):
        att_copy(k).start()
    for n in range(2):
        for k in range(seq // 2, seq):
            g_copy(k, n).wait_recv()

    def spread(block, j):
        if j < 2:
            return block[:patch, j * HEAD_DIM : (j + 1) * HEAD_DIM]
        piece = block[patch + (j - 2) * half_patch : patch + (j - 1) * half_patch]
        return jnp.concatenate([piece[:, :HEAD_DIM], piece[:, HEAD_DIM:]], axis=0)

    back = jnp.zeros((patch, depth), jnp.float32)
    for j in range(3):
        both = [spread(ref[t], j) for t in range(seq) for ref in (gall, glast)]
        back = back + mm(jnp.concatenate(both, axis=1), weight[j], NT)
    outer = spread(glast[0], 3).astype(jnp.float32)
    for t in range(1, seq):
        outer = outer + spread(glast[t], 3).astype(jnp.float32)
    a_high, a_low = split2(outer)
    embed_low = embed_ref[:, own_cols]
    back = back * gain_own - (mm(a_high, embed_low) + mm(a_low, embed_low))
    rows = patch // (2 * groups)
    part[...] = back.reshape(2 * groups, rows, depth)
    rpeers = [(dg, dh) for dg in range(groups) for dh in range(2) if dg + dh]

    def r_copy(i):
        dg, dh = rpeers[i]
        og, oh = lax.rem(g + dg, groups), lax.rem(h + dh, 2)
        return remote(part.at[og * 2 + oh], rrecv.at[i], r_send.at[i], r_recv.at[i], (og, s, oh))

    for i in range(len(rpeers)):
        r_copy(i).start()
    index = g * 2 + h
    done = part[index]
    for i in range(len(rpeers)):
        r_copy(i).wait_recv()
        done = done + rrecv[i]
    quarter[...] = done.astype(jnp.bfloat16)

    half = seq // 2
    owner = s // half
    slot = index * half + lax.rem(s, half)
    place = gathered.at[
        pl.ds(pl.multiple_of(index * rows, 16), rows), pl.ds(pl.multiple_of(lax.rem(s, half) * depth, 128), depth)
    ]

    def f_copy(k):
        dg, ds = k // seq, k % seq
        return remote(quarter, place, f_send.at[k], f_recv.at[slot], (lax.rem(g + dg, groups), far(ds), owner))

    local = pltpu.make_async_copy(quarter, place, f_local)
    for k in sorted(range(1, groups * seq), key=lambda k: abs(k % seq - seq // 2)):
        f_copy(k).start()
    pl.when(owner != h)(lambda: f_copy(0).start())
    pl.when(owner == h)(lambda: local.start())

    def f_arrival(i):
        there = gathered.at[(i // half) * rows : (i // half + 1) * rows, (i % half) * depth : (i % half + 1) * depth]
        return remote(quarter, there, f_send.at[0], f_recv.at[i], (g, s, h))

    for k in range(1, seq):
        order_copy(k).wait_send()
        cot_copy(k).wait_send()
        m_copy(k).wait_send()
        g_copy(k, 0).wait_send()
        g_copy(k, 1).wait_send()
        att_copy(k).wait_send()
        att_copy(k).wait_recv()
    halo_copy(0).wait_send()
    for i in range(1, 5):
        pl.when(s + hops[i][0] < seq)(lambda i=i: halo_copy(i).wait_send())
    for i in range(len(peers)):
        lat_copy(i).wait_send()
    for i in range(len(rpeers)):
        r_copy(i).wait_send()
    for k in range(1, groups * seq):
        f_copy(k).wait_send()
    pl.when(owner != h)(lambda: f_copy(0).wait_send())
    pl.when(owner == h)(lambda: local.wait())
    for i in range(2 * groups * half):
        pl.when(jnp.logical_or(owner != h, slot != i))(lambda i=i: f_arrival(i).wait_recv())
    grad_ref[...] = gathered[...].astype(jnp.float32)


def fast_device(groups, seq, *operands):
    features, conv_weight, conv_bias, token_order, embed_weight, norm_gain, qkv_weight, grad_out = operands
    channels, lat_ch = conv_weight.shape[-2:]
    depth, _, width = qkv_weight.shape
    patch, model = embed_weight.shape
    own_rows = token_order.shape[0]
    cols = width // seq
    block = features.shape[2] * features.shape[3] // 4
    f32, b16 = jnp.float32, jnp.bfloat16
    vmem = pl.BlockSpec(memory_space=pltpu.VMEM)
    dma = pltpu.SemaphoreType.DMA
    rows = patch // (2 * groups)
    pairs = [7, 3] + [seq - 1] * 6 + [5] * 2 + [2 * seq - 1] * 2 + [seq - 1] * 6 + [2 * groups - 1] * 2 + [groups * seq] * 2
    attended, embed_grad = pl.pallas_call(
        functools.partial(fused, groups, seq),
        out_shape=(
            jax.ShapeDtypeStruct((own_rows, width), b16),
            jax.ShapeDtypeStruct((patch, model // 2), f32),
        ),
        in_specs=[pl.BlockSpec(memory_space=pltpu.HBM)] * 8,
        out_specs=(vmem, vmem),
        scratch_shapes=[
            pltpu.VMEM((4 * block, channels), b16),
            pltpu.VMEM((27 * lat_ch, channels), b16),
            pltpu.VMEM((1, lat_ch), f32),
            pltpu.VMEM((1, own_rows), jnp.int32),
            pltpu.VMEM((patch, model), b16),
            pltpu.VMEM((1, model), f32),
            pltpu.VMEM((own_rows, width), b16),
            pltpu.VMEM((3, depth, width), b16),
            pltpu.VMEM((seq, 3, patch, cols), b16),
            pltpu.VMEM((seq - 1, 3, patch, cols), b16),
            pltpu.VMEM((seq, own_rows, cols), b16),
            pltpu.VMEM((seq, 1, own_rows), jnp.int32),
            pltpu.VMEM((3, block, patch), f32),
            pltpu.VMEM((3, block, patch), f32),
            pltpu.VMEM((5, block, patch), f32),
            pltpu.VMEM((block, patch), f32),
            pltpu.VMEM((2 * seq, block, patch), b16),
            pltpu.VMEM((seq, own_rows, cols), b16),
            pltpu.VMEM((seq, 3 * patch // 2, 2 * HEAD_DIM), b16),
            pltpu.VMEM((seq, 2 * patch, 2 * HEAD_DIM), b16),
            pltpu.VMEM((2 * groups, rows, depth), f32),
            pltpu.VMEM((2 * groups - 1, rows, depth), f32),
            pltpu.VMEM((rows, depth), b16),
            pltpu.VMEM((patch, model // 2), b16),
        ]
        + [dma((n,)) for n in pairs]
        + [dma],
        compiler_params=pltpu.CompilerParams(collective_id=0, has_side_effects=True),
    )(
        features.reshape(4 * block, channels),
        jnp.transpose(conv_weight, (0, 1, 2, 4, 3)).reshape(-1, channels),
        conv_bias.reshape(1, lat_ch),
        token_order.reshape(1, own_rows),
        embed_weight,
        norm_gain.reshape(1, model),
        jnp.transpose(qkv_weight, (1, 0, 2)),
        grad_out[0],
    )
    return attended[None], embed_grad


def fits(mesh, features, conv_weight, embed_weight, qkv_weight, token_order):
    groups, seq, heads = (mesh.shape[axis] for axis in ("grp", "seq", "head"))
    clips, frames, rows, columns, _ = features.shape
    width = qkv_weight.shape[2] // heads
    depth = qkv_weight.shape[0] // seq
    patch = embed_weight.shape[0]
    return (
        heads == 2
        and clips == groups
        and frames == seq
        and seq % 2 == 0
        and rows == 2 * heads
        and columns % 32 == 0
        and width == seq * 2 * HEAD_DIM
        and depth % 128 == 0
        and patch == 4 * conv_weight.shape[-1]
        and patch == HEAD_DIM
        and patch % (16 * groups) == 0
        and token_order.shape[0] == seq * columns
        and token_order.shape[0] % (16 * seq) == 0
    )


def solution(mesh):
    placed = (
        P("grp", "seq", "head", None, None),
        P(),
        P(),
        P("seq"),
        P(),
        P(),
        P("seq", None, "head"),
        P("grp", "seq", "head"),
    )

    def run(features, conv_weight, conv_bias, token_order, embed_weight, norm_gain, qkv_weight, grad_out):
        body = per_device
        if fits(mesh, features, conv_weight, embed_weight, qkv_weight, token_order):
            body = functools.partial(fast_device, mesh.shape["grp"], mesh.shape["seq"])
        return jax.shard_map(
            body,
            mesh=mesh,
            in_specs=placed,
            out_specs=(P("grp", "seq", "head"), P(None, "head")),
            check_vma=False,
        )(features, conv_weight, conv_bias, token_order, embed_weight, norm_gain, qkv_weight, grad_out)

    return run
```

profile of v0, /device:TPU:1, one launch (start us, length us, event | category | flops | bytes accessed | tf_op | source)
XLA Modules:
  0.0 50.5 jit_solution(13118271030767007216)
XLA Ops:
  0.6 46.6 %shard_map.95 = (bf16[32,1024]{1,0:T(8,128)(2,1)}, f32[64,1536]{1,0:T(8,128)}) custom-call(bf16[64,512]{1,0:T(8,128)(2,1)} %bitcast.12, bf16[432,512]{1,0:T(8,128)(2,1)} %bitcast.11, f32[1,16]{1,0:T(1,128)} %bitcast.16, s32[1,32]{1,0:T(1,128)} %bitcast.17, bf16[64,3072]{1,0:T(8,128)(2,1)} %embed_hbm.1, f32[1,3072]{1,0:T(1,128)} %bitcast.15, ...), custom_call_target="tpu_custom_call" | custom-call | tf_op jit(solution)/shard_map/pallas_call | solution.py:554
  47.2 1.5 %copy.12 = bf16[1,32,1024]{2,1,0:T(8,128)(2,1)} copy(bf16[1,32,1024]{2,1,0:T(8,128)(2,1)} %bitcast.14) | data formatting | bytes 131072
  48.7 1.8 %copy.13 = f32[64,1536]{1,0:T(8,128)} copy(f32[64,1536]{1,0:T(8,128)} %get-tuple-element.9) | data formatting | bytes 786432
where the time goes:
time: 50.7 us; the launch traced here: 50.5 us
  Pallas kernels  46.6 us (92%)
  local copies, waits for them, and re-layouts  3.24 us (6%)
  between operations  0.64 us (1%)
    pallas_call x1, Pallas kernels, fast_device(): pl.pallas_call(functools.partial(fused, groups, seq), out_shape=(jax.Shap...  46.6 us
    unnamed x2, local copies, waits for them, and re-layouts  3.24 us

commit v1 on v0

--- a/solution.py
+++ b/solution.py
@@ -203,32 +203,29 @@
     groups, seq, feat_hbm, conv_hbm, bias_hbm, order_hbm, embed_hbm, gain_hbm, weight_hbm, cot_hbm,
     att_ref, grad_ref,
     feat_ref, conv_ref, bias_ref, order_ref, embed_ref, gain_ref, cot_ref,
-    weight, mbuf, mrecv, cots, orders, halo_own, halo_par, halo_in, lat_acc, patches, att,
-    gall, glast, part, rrecv, quarter, gathered,
+    weight, mbuf, mrecv, cotpack, cots, orders, halo_own, halo_par, halo_in, lat_acc, patches, att, attin,
+    hot_ref, gall, part, rrecv, quarter, gathered,
     in_sem, w_sem, m_send, m_recv, c_send, c_recv, o_send, o_recv, h_send, h_recv, l_send, l_recv,
-    t_send, t_recv, g_send, g_recv, b_send, b_recv, r_send, r_recv, f_send, f_recv, f_local,
+    t_send, t_recv, g_send, g_recv, r_send, r_recv, f_send, f_recv, f_local,
 ):
     g, s, h = lax.axis_index("grp"), lax.axis_index("seq"), lax.axis_index("head")
     own_rows = cot_ref.shape[0]
+    half_rows = own_rows // 2
     tokens_all = own_rows * seq
     depth = weight.shape[1]
-    cols = att.shape[2]
+    cols = weight.shape[2]
     patch = embed_ref.shape[0]
+    half_patch = patch // 2
     width_model = embed_ref.shape[1]
     lat_ch = bias_ref.shape[1]
-    wide = 3 * cols
+    pair = 2 * HEAD_DIM
     far = lambda off: lax.rem(s + off, seq)
-
-    barrier = pltpu.get_barrier_semaphore()
-    for dg in range(groups):
-        for ds in range(seq):
-            for dh in range(2):
-                if dg + ds + dh:
-                    pl.semaphore_signal(
-                        barrier, inc=1, device_id=(lax.rem(g + dg, groups), far(ds), lax.rem(h + dh, 2)),
-                        device_id_type=MESH,
-                    )
-    w_copies = [pltpu.make_async_copy(weight_hbm.at[j], weight.at[j], w_sem.at[j]) for j in range(3)]
+    other = lambda off: lax.rem(g + off, groups)
+
+    here_cols = pl.ds(pl.multiple_of(g * cols, 128), cols)
+    w_copies = [
+        pltpu.make_async_copy(weight_hbm.at[j, :, here_cols], weight.at[j], w_sem.at[j]) for j in range(3)
+    ]
     in_copies = [
         pltpu.make_async_copy(src, dst, in_sem.at[i])
         for i, (src, dst) in enumerate(
@@ -240,6 +237,15 @@
     ]
     for c in in_copies + w_copies:
         c.start()
+    barrier = pltpu.get_barrier_semaphore()
+    everyone = [
+        (dg, ds, dh) for ds in sorted(range(seq), key=lambda k: abs(k - seq // 2)) for dg in range(groups)
+        for dh in range(2) if dg + ds + dh
+    ]
+    for dg, ds, dh in everyone:
+        pl.semaphore_signal(
+            barrier, inc=1, device_id=(other(dg), far(ds), lax.rem(h + dh, 2)), device_id_type=MESH
+        )
     in_copies[0].wait()
     in_copies[1].wait()
 
@@ -283,48 +289,62 @@
         halo_own[a] = jnp.concatenate([x[:, lanes] for x in own], axis=1)
         halo_par[a] = jnp.concatenate([x[:, lanes] for x in par], axis=1)
 
+    pl.semaphore_wait(barrier, 2 * groups * seq - 1)
+
+    hops = [(0, 1, halo_par, 2), (1, 0, halo_own, 1), (1, 1, halo_par, 1), (2, 0, halo_own, 0), (2, 1, halo_par, 0)]
+
+    def halo_copy(i):
+        ds, dh, src, a = hops[i]
+        return remote(
+            src.at[a], halo_in.at[i], h_send.at[i], h_recv.at[i], (g, lax.rem(s + ds, seq), lax.rem(h + dh, 2))
+        )
+
+    halo_copy(0).start()
+    for i in range(1, 5):
+        pl.when(s + hops[i][0] < seq)(lambda i=i: halo_copy(i).start())
+
     for c in in_copies[2:]:
         c.wait()
+
+    def order_copy(k):
+        return remote(order_ref, orders.at[s], o_send.at[k - 1], o_recv.at[k - 1], (g, far(k), h))
+
+    for k in range(1, seq):
+        order_copy(k).start()
+    orders[s] = order_ref[...]
+
+    for i in range(groups * seq // 2):
+        two = cot_ref[:, i * pair : (i + 1) * pair]
+        for n in range(2):
+            one = two[:, n * HEAD_DIM : (n + 1) * HEAD_DIM]
+            cotpack[2 * i + n] = jnp.concatenate([one[:half_rows], one[half_rows:]], axis=1)
+    mine = g * seq + s
+    spots = [(dg, ds) for dg in range(groups) for ds in range(seq) if dg + ds]
+
+    def cot_copy(k):
+        dg, ds = spots[k]
+        return remote(
+            cotpack.at[other(dg) * seq + far(ds)], cots.at[mine], c_send.at[k], c_recv.at[k], (other(dg), far(ds), h)
+        )
+
+    for k in range(len(spots)):
+        cot_copy(k).start()
+    cots[mine] = cotpack[mine]
+
     own_cols = pl.ds(pl.multiple_of(s * depth, 128), depth)
     embed_own = embed_ref[:, own_cols].astype(jnp.float32)
     gain_own = gain_ref[:, own_cols]
     eg_high, eg_low = split2(embed_own * gain_own)
     eg = jnp.concatenate([eg_high, eg_low], axis=0)
-
-    pl.semaphore_wait(barrier, 2 * groups * seq - 1)
-
-    hops = [(0, 1, halo_par, 2), (1, 0, halo_own, 1), (1, 1, halo_par, 1), (2, 0, halo_own, 0), (2, 1, halo_par, 0)]
-
-    def halo_copy(i):
-        ds, dh, src, a = hops[i]
-        return remote(
-            src.at[a], halo_in.at[i], h_send.at[i], h_recv.at[i], (g, lax.rem(s + ds, seq), lax.rem(h + dh, 2))
-        )
-
-    halo_copy(0).start()
-    for i in range(1, 5):
-        pl.when(s + hops[i][0] < seq)(lambda i=i: halo_copy(i).start())
-
-    def order_copy(k):
-        return remote(order_ref, orders.at[s], o_send.at[k - 1], o_recv.at[k - 1], (g, far(k), h))
-
-    def cot_copy(k):
-        return remote(
-            cot_ref.at[:, pl.ds(pl.multiple_of(far(k) * cols, 128), cols)], cots.at[s],
-            c_send.at[k - 1], c_recv.at[k - 1], (g, far(k), h),
-        )
-
-    for k in range(1, seq):
-        order_copy(k).start()
-    orders[s] = order_ref[...]
-    cots[s] = cot_ref[:, pl.ds(pl.multiple_of(s * cols, 128), cols)]
-
+    prods = []
     for j in range(3):
         w_copies[j].wait()
         prod = mm(eg, weight[j])
-        prod = prod[:patch] + prod[patch:]
-        for t in range(seq):
-            mbuf[t, j] = prod[:, t * cols : (t + 1) * cols].astype(jnp.bfloat16)
+        prods.append(prod[:patch] + prod[patch:])
+    for t in range(seq):
+        q, k, v = (x[:, t * HEAD_DIM : (t + 1) * HEAD_DIM] for x in prods)
+        mbuf[t, :patch] = jnp.concatenate([q, k], axis=1).astype(jnp.bfloat16)
+        mbuf[t, patch:] = jnp.concatenate([v[:half_patch], v[half_patch:]], axis=1).astype(jnp.bfloat16)
 
     def m_copy(k):
         return remote(mbuf.at[far(k)], mrecv.at[k - 1], m_send.at[k - 1], m_recv.at[k - 1], (g, far(k), h))
@@ -342,79 +362,69 @@
             lat_acc[...] += halo_in[i]
 
         pl.when(s >= hops[i][0])(add)
-    mine = 2 * s + h
-    patches[mine] = lat_acc[...].astype(jnp.bfloat16)
-    peers = [(ds, dh) for ds in range(seq) for dh in range(2) if ds + dh]
+    lat_at = (g * seq + s) * 2 + h
+    patches[lat_at] = lat_acc[...].astype(jnp.bfloat16)
 
     def lat_copy(i):
-        ds, dh = peers[i]
+        dg, ds, dh = everyone[i]
         return remote(
-            patches.at[mine], patches.at[mine], l_send.at[i], l_recv.at[i], (g, far(ds), lax.rem(h + dh, 2))
-        )
-
-    for i in range(len(peers)):
+            patches.at[lat_at], patches.at[lat_at], l_send.at[i], l_recv.at[i],
+            (other(dg), far(ds), lax.rem(h + dh, 2)),
+        )
+
+    for i in range(len(everyone)):
         lat_copy(i).start()
     for k in far_first[seq // 2 :]:
         m_copy(k).start()
-    for k in range(1, seq):
-        cot_copy(k).start()
 
     for k in range(1, seq):
         order_copy(k).wait_recv()
-    hot = jnp.concatenate(
-        [
-            jnp.where(
-                lax.broadcasted_iota(jnp.int32, (tokens_all, own_rows), 0) == orders[t][:1], 1.0, 0.0
-            )
-            for t in range(seq)
-        ],
-        axis=1,
-    ).astype(jnp.bfloat16)
-
-    for i in range(len(peers)):
+    row = jnp.concatenate([orders[t][:1] for t in range(seq)], axis=1).astype(jnp.float32)
+    spread_order = jnp.transpose(jnp.broadcast_to(row, (128, tokens_all)))
+    lane = lax.broadcasted_iota(jnp.int32, (tokens_all, 128), 1).astype(jnp.float32)
+    for i in range(tokens_all // 128):
+        hot_ref[:, i * 128 : (i + 1) * 128] = jnp.where(spread_order == lane + float(i * 128), 1.0, 0.0).astype(
+            jnp.bfloat16
+        )
+    gram = mm(embed_ref[...], embed_ref[...], NT)
+    gram_high, gram_rest = split2(gram)
+    gram_mid, gram_low = split2(gram - gram_high.astype(jnp.float32))
+    for k in range(len(spots)):
+        cot_copy(k).wait_recv()
+
+    for i in range(len(everyone)):
         lat_copy(i).wait_recv()
-    tokens = mm(hot, patches[...].reshape(tokens_all, patch), TN).astype(jnp.bfloat16)
-    square = jnp.zeros((tokens_all, 1), jnp.float32)
-    chunk = depth
-    for t in range(width_model // chunk):
-        mixed = mm(tokens, embed_ref[:, t * chunk : (t + 1) * chunk])
-        square = square + jnp.sum(mixed * mixed, axis=-1, keepdims=True)
-    inverse = lax.rsqrt(square / width_model + 1e-06)
-
-    total = [mbuf[s, j].astype(jnp.float32) for j in range(3)]
+    tokens, inverse = [], []
+    for c in range(groups):
+        own_patches = patches[c * 2 * seq : (c + 1) * 2 * seq].reshape(tokens_all, patch)
+        made = mm(hot_ref[...], own_patches)
+        tok = made.astype(jnp.bfloat16)
+        square = mm(tok, gram_high) + mm(tok, gram_mid) + mm(tok, gram_low)
+        square = jnp.sum(square * made, axis=-1, keepdims=True)
+        tokens.append(tok)
+        inverse.append(lax.rsqrt(square / width_model + 1e-06))
+
+    total = mbuf[s].astype(jnp.float32)
     for k in range(1, seq):
         m_copy(k).wait_recv()
-        total = [total[j] + mrecv[k - 1, j].astype(jnp.float32) for j in range(3)]
-    m_high, m_low = split2(jnp.concatenate(total, axis=1))
-    proj = (mm(tokens, m_high) + mm(tokens, m_low)) * inverse
-    low = proj.astype(jnp.bfloat16)
-
-    for k in range(1, seq):
-        cot_copy(k).wait_recv()
-    cot_all = cots[...].reshape(tokens_all, cols)
+        total = total + mrecv[k - 1].astype(jnp.float32)
+    total = jnp.concatenate(
+        [total[:patch], jnp.concatenate([total[patch:, :HEAD_DIM], total[patch:, HEAD_DIM:]], axis=0)], axis=1
+    )
+    m_high, m_low = split2(total)
+
     factor = HEAD_DIM ** (-0.5)
-    half_patch = patch // 2
-    scaled_tokens = tokens.astype(jnp.float32) * (inverse * inverse / width_model)
+    made = jnp.zeros((patch, 4 * HEAD_DIM), jnp.float32)
     outs = []
-    inner = jnp.zeros((tokens_all, 1), jnp.float32)
-
-    beside = s + 1 - 2 * lax.rem(s, 2)
-
-    def g_copy(k, n):
-        blocks, send, recv = (gall, g_send, g_recv) if n == 0 else (glast, b_send, b_recv)
-        hop = seq // 2
-        if k < hop:
-            source, to = s, far(2 * k)
-        elif k == hop:
-            source, to = s, beside
-        else:
-            source, to = far(seq - 2 * (k - hop)), beside
-        return remote(blocks.at[source], blocks.at[source], send.at[k - 1], recv.at[k - 1], (g, to, h))
-
-    for n in range(2):
-        lanes = lambda j: slice(j * cols + n * HEAD_DIM, j * cols + (n + 1) * HEAD_DIM)
+    for c in range(groups):
+        tok, inv = tokens[c], inverse[c]
+        proj = (mm(tok, m_high) + mm(tok, m_low)) * inv
+        low = proj.astype(jnp.bfloat16)
+        lanes = lambda j: slice(j * HEAD_DIM, (j + 1) * HEAD_DIM)
         query, keys, values = low[:, lanes(0)], low[:, lanes(1)], low[:, lanes(2)]
-        cotan = cot_all[:, lanes(0)]
+        cotan = jnp.concatenate(
+            [cots[c * seq + t][:, lanes(n)] for t in range(seq) for n in range(2)], axis=0
+        )
         scores = mm(query, keys, NT) * factor
         top = jnp.max(scores, axis=-1, keepdims=True)
         expd = jnp.exp(scores - top)
@@ -427,37 +437,53 @@
         outs.append(output)
         parts = [mm(dscore, keys) * factor, mm(dscore, query, TN) * factor, mm(probs_low, cotan, TN)]
         parts = [x.astype(jnp.bfloat16).astype(jnp.float32) for x in parts]
+        inner = jnp.zeros((tokens_all, 1), jnp.float32)
         for j in range(3):
             inner = inner + jnp.sum(parts[j] * proj[:, lanes(j)], axis=-1, keepdims=True)
-        rhs = [x * inverse for x in parts]
-        if n == 1:
-            rhs.append(scaled_tokens * inner)
+        rhs = [x * inv for x in parts] + [tok.astype(jnp.float32) * (inv * inv / width_model * inner)]
         rhs_high, rhs_low = split2(jnp.concatenate(rhs, axis=1))
-        made = mm(tokens, rhs_high, TN) + mm(tokens, rhs_low, TN)
-        packed = [made[:, : 2 * HEAD_DIM]]
-        for j in range(2, len(rhs)):
-            piece = made[:, j * HEAD_DIM : (j + 1) * HEAD_DIM]
-            packed.append(jnp.concatenate([piece[:half_patch], piece[half_patch:]], axis=1))
-        (gall if n == 0 else glast)[s] = jnp.concatenate(packed, axis=0).astype(jnp.bfloat16)
-        for k in range(1, seq // 2 + 1):
-            g_copy(k, n).start()
-    att[...] = jnp.concatenate(outs, axis=1).reshape(seq, own_rows, cols)
-    here = pl.ds(pl.multiple_of(s * cols, 128), cols)
+        made = made + (mm(tok, rhs_high, TN) + mm(tok, rhs_low, TN))
+    packed = [made[:, :pair]]
+    for j in range(2, 4):
+        piece = made[:, j * HEAD_DIM : (j + 1) * HEAD_DIM]
+        packed.append(jnp.concatenate([piece[:half_patch], piece[half_patch:]], axis=1))
+    gall[s] = jnp.concatenate(packed, axis=0).astype(jnp.bfloat16)
+
+    beside = s + 1 - 2 * lax.rem(s, 2)
+    hop = seq // 2
+
+    def g_copy(k):
+        if k < hop:
+            source, to = s, far(2 * k)
+        elif k == hop:
+            source, to = s, beside
+        else:
+            source, to = far(seq - 2 * (k - hop)), beside
+        return remote(gall.at[source], gall.at[source], g_send.at[k - 1], g_recv.at[k - 1], (g, to, h))
+
+    for k in range(1, hop + 1):
+        g_copy(k).start()
+
+    for c in range(groups):
+        for t in range(seq):
+            one = outs[c][t * own_rows : (t + 1) * own_rows]
+            att[c * seq + t] = jnp.concatenate([one[:half_rows], one[half_rows:]], axis=1)
 
     def att_copy(k):
-        return remote(att.at[far(k)], att_ref.at[:, here], t_send.at[k - 1], t_recv.at[k - 1], (g, far(k), h))
-
-    att_ref[:, here] = att[s]
-
-    for n in range(2):
-        for k in range(1, seq // 2):
-            g_copy(k, n).wait_recv()
-            g_copy(seq // 2 + k, n).start()
-    for k in range(1, seq):
+        dg, ds = spots[k]
+        return remote(
+            att.at[other(dg) * seq + far(ds)], attin.at[mine], t_send.at[k], t_recv.at[k], (other(dg), far(ds), h)
+        )
+
+    attin[mine] = att[mine]
+
+    for k in range(1, hop):
+        g_copy(k).wait_recv()
+        g_copy(hop + k).start()
+    for k in range(len(spots)):
         att_copy(k).start()
-    for n in range(2):
-        for k in range(seq // 2, seq):
-            g_copy(k, n).wait_recv()
+    for k in range(hop, seq):
+        g_copy(k).wait_recv()
 
     def spread(block, j):
         if j < 2:
@@ -467,11 +493,11 @@
 
     back = jnp.zeros((patch, depth), jnp.float32)
     for j in range(3):
-        both = [spread(ref[t], j) for t in range(seq) for ref in (gall, glast)]
-        back = back + mm(jnp.concatenate(both, axis=1), weight[j], NT)
-    outer = spread(glast[0], 3).astype(jnp.float32)
+        all_heads = jnp.concatenate([spread(gall[t], j) for t in range(seq)], axis=1)
+        back = back + mm(all_heads, weight[j], NT)
+    outer = spread(gall[0], 3).astype(jnp.float32)
     for t in range(1, seq):
-        outer = outer + spread(glast[t], 3).astype(jnp.float32)
+        outer = outer + spread(gall[t], 3).astype(jnp.float32)
     a_high, a_low = split2(outer)
     embed_low = embed_ref[:, own_cols]
     back = back * gain_own - (mm(a_high, embed_low) + mm(a_low, embed_low))
@@ -481,7 +507,7 @@
 
     def r_copy(i):
         dg, dh = rpeers[i]
-        og, oh = lax.rem(g + dg, groups), lax.rem(h + dh, 2)
+        og, oh = other(dg), lax.rem(h + dh, 2)
         return remote(part.at[og * 2 + oh], rrecv.at[i], r_send.at[i], r_recv.at[i], (og, s, oh))
 
     for i in range(len(rpeers)):
@@ -502,7 +528,7 @@
 
     def f_copy(k):
         dg, ds = k // seq, k % seq
-        return remote(quarter, place, f_send.at[k], f_recv.at[slot], (lax.rem(g + dg, groups), far(ds), owner))
+        return remote(quarter, place, f_send.at[k], f_recv.at[slot], (other(dg), far(ds), owner))
 
     local = pltpu.make_async_copy(quarter, place, f_local)
     for k in sorted(range(1, groups * seq), key=lambda k: abs(k % seq - seq // 2)):
@@ -514,18 +540,25 @@
         there = gathered.at[(i // half) * rows : (i // half + 1) * rows, (i % half) * depth : (i % half + 1) * depth]
         return remote(quarter, there, f_send.at[0], f_recv.at[i], (g, s, h))
 
+    for k in range(len(spots)):
+        att_copy(k).wait_recv()
+    for i in range(groups * seq // 2):
+        both = [attin[2 * i], attin[2 * i + 1]]
+        for n in range(2):
+            att_ref[n * half_rows : (n + 1) * half_rows, i * pair : (i + 1) * pair] = jnp.concatenate(
+                [x[:, n * HEAD_DIM : (n + 1) * HEAD_DIM] for x in both], axis=1
+            )
     for k in range(1, seq):
         order_copy(k).wait_send()
+        m_copy(k).wait_send()
+        g_copy(k).wait_send()
+    for k in range(len(spots)):
         cot_copy(k).wait_send()
-        m_copy(k).wait_send()
-        g_copy(k, 0).wait_send()
-        g_copy(k, 1).wait_send()
         att_copy(k).wait_send()
-        att_copy(k).wait_recv()
     halo_copy(0).wait_send()
     for i in range(1, 5):
         pl.when(s + hops[i][0] < seq)(lambda i=i: halo_copy(i).wait_send())
-    for i in range(len(peers)):
+    for i in range(len(everyone)):
         lat_copy(i).wait_send()
     for i in range(len(rpeers)):
         r_copy(i).wait_send()
@@ -544,13 +577,19 @@
     depth, _, width = qkv_weight.shape
     patch, model = embed_weight.shape
     own_rows = token_order.shape[0]
-    cols = width // seq
+    cols = width // groups
     block = features.shape[2] * features.shape[3] // 4
+    tokens_all = own_rows * seq
+    pair = 2 * HEAD_DIM
     f32, b16 = jnp.float32, jnp.bfloat16
     vmem = pl.BlockSpec(memory_space=pltpu.VMEM)
     dma = pltpu.SemaphoreType.DMA
     rows = patch // (2 * groups)
-    pairs = [7, 3] + [seq - 1] * 6 + [5] * 2 + [2 * seq - 1] * 2 + [seq - 1] * 6 + [2 * groups - 1] * 2 + [groups * seq] * 2
+    spots, everyone = groups * seq, 2 * groups * seq
+    pairs = (
+        [7, 3] + [seq - 1] * 2 + [spots - 1] * 2 + [seq - 1] * 2 + [5] * 2 + [everyone - 1] * 2 + [spots - 1] * 2
+        + [seq - 1] * 2 + [2 * groups - 1] * 2 + [spots] * 2
+    )
     attended, embed_grad = pl.pallas_call(
         functools.partial(fused, groups, seq),
         out_shape=(
@@ -567,19 +606,21 @@
             pltpu.VMEM((patch, model), b16),
             pltpu.VMEM((1, model), f32),
             pltpu.VMEM((own_rows, width), b16),
-            pltpu.VMEM((3, depth, width), b16),
-            pltpu.VMEM((seq, 3, patch, cols), b16),
-            pltpu.VMEM((seq - 1, 3, patch, cols), b16),
-            pltpu.VMEM((seq, own_rows, cols), b16),
+            pltpu.VMEM((3, depth, cols), b16),
+            pltpu.VMEM((seq, 3 * patch // 2, pair), b16),
+            pltpu.VMEM((seq - 1, 3 * patch // 2, pair), b16),
+            pltpu.VMEM((spots, own_rows // 2, pair), b16),
+            pltpu.VMEM((spots, own_rows // 2, pair), b16),
             pltpu.VMEM((seq, 1, own_rows), jnp.int32),
             pltpu.VMEM((3, block, patch), f32),
             pltpu.VMEM((3, block, patch), f32),
             pltpu.VMEM((5, block, patch), f32),
             pltpu.VMEM((block, patch), f32),
-            pltpu.VMEM((2 * seq, block, patch), b16),
-            pltpu.VMEM((seq, own_rows, cols), b16),
-            pltpu.VMEM((seq, 3 * patch // 2, 2 * HEAD_DIM), b16),
-            pltpu.VMEM((seq, 2 * patch, 2 * HEAD_DIM), b16),
+            pltpu.VMEM((everyone, block, patch), b16),
+            pltpu.VMEM((spots, own_rows // 2, pair), b16),
+            pltpu.VMEM((spots, own_rows // 2, pair), b16),
+            pltpu.VMEM((tokens_all, tokens_all), b16),
+            pltpu.VMEM((seq, 2 * patch, pair), b16),
             pltpu.VMEM((2 * groups, rows, depth), f32),
             pltpu.VMEM((2 * groups - 1, rows, depth), f32),
             pltpu.VMEM((rows, depth), b16),
@@ -614,13 +655,15 @@
         and seq % 2 == 0
         and rows == 2 * heads
         and columns % 32 == 0
-        and width == seq * 2 * HEAD_DIM
+        and width == groups * seq * HEAD_DIM
+        and (seq * HEAD_DIM) % 128 == 0
         and depth % 128 == 0
         and patch == 4 * conv_weight.shape[-1]
         and patch == HEAD_DIM
         and patch % (16 * groups) == 0
         and token_order.shape[0] == seq * columns
-        and token_order.shape[0] % (16 * seq) == 0
+        and token_order.shape[0] % (32 * seq) == 0
+        and token_order.shape[0] % 128 == 0
     )
 
 

time: 50.7 us -> 45.6 us (0.90)
  Pallas kernels: 46.6 us -> 41.5 us
    pallas_call x1, Pallas kernels: 46.6 us -> 41.5 us  [fast_device(): pl.pallas_call(functools.partial(fused, groups, seq), out_shape=(jax.Shap...]
where the time goes in v1:
time: 45.6 us; the launch traced here: 45.4 us
  Pallas kernels  41.5 us (91%)
  local copies, waits for them, and re-layouts  3.24 us (7%)
  between operations  0.64 us (1%)
    pallas_call x1, Pallas kernels, fast_device(): pl.pallas_call(functools.partial(fused, groups, seq), out_shape=(jax.Shap...  41.5 us
    unnamed x2, local copies, waits for them, and re-layouts  3.24 us

profile of v1, /device:TPU:1, one launch (start us, length us, event | category | flops | bytes accessed | tf_op | source)
XLA Modules:
  0.0 45.4 jit_solution(16438127050765568240)
XLA Ops:
  0.6 41.5 %shard_map.95 = (bf16[32,1024]{1,0:T(8,128)(2,1)}, f32[64,1536]{1,0:T(8,128)}) custom-call(bf16[64,512]{1,0:T(8,128)(2,1)} %bitcast.12, bf16[432,512]{1,0:T(8,128)(2,1)} %bitcast.11, f32[1,16]{1,0:T(1,128)} %bitcast.16, s32[1,32]{1,0:T(1,128)} %bitcast.17, bf16[64,3072]{1,0:T(8,128)(2,1)} %embed_hbm.1, f32[1,3072]{1,0:T(1,128)} %bitcast.15, ...), custom_call_target="tpu_custom_call" | custom-call | tf_op jit(solution)/shard_map/pallas_call | solution.py:593
  42.2 1.5 %copy.12 = bf16[1,32,1024]{2,1,0:T(8,128)(2,1)} copy(bf16[1,32,1024]{2,1,0:T(8,128)(2,1)} %bitcast.14) | data formatting | bytes 131072
  43.7 1.8 %copy.13 = f32[64,1536]{1,0:T(8,128)} copy(f32[64,1536]{1,0:T(8,128)} %get-tuple-element.9) | data formatting | bytes 786432

commit v2 on v1

--- a/solution.py
+++ b/solution.py
@@ -568,7 +568,12 @@
     pl.when(owner == h)(lambda: local.wait())
     for i in range(2 * groups * half):
         pl.when(jnp.logical_or(owner != h, slot != i))(lambda i=i: f_arrival(i).wait_recv())
-    grad_ref[...] = gathered[...].astype(jnp.float32)
+    grad_ref[...] = gathered[...]
+
+
+def finish(att_in, grad_in, att_out, grad_out):
+    att_out[...] = att_in[...]
+    grad_out[...] = grad_in[...].astype(jnp.float32)
 
 
 def fast_device(groups, seq, *operands):
@@ -593,8 +598,8 @@
     attended, embed_grad = pl.pallas_call(
         functools.partial(fused, groups, seq),
         out_shape=(
-            jax.ShapeDtypeStruct((own_rows, width), b16),
-            jax.ShapeDtypeStruct((patch, model // 2), f32),
+            pltpu.VMEM((own_rows, width), b16),
+            pltpu.VMEM((patch, model // 2), b16),
         ),
         in_specs=[pl.BlockSpec(memory_space=pltpu.HBM)] * 8,
         out_specs=(vmem, vmem),
@@ -639,6 +644,16 @@
         jnp.transpose(qkv_weight, (1, 0, 2)),
         grad_out[0],
     )
+    attended, embed_grad = pl.pallas_call(
+        finish,
+        out_shape=(
+            jax.ShapeDtypeStruct((own_rows, width), b16),
+            jax.ShapeDtypeStruct((patch, model // 2), f32),
+        ),
+        in_specs=[vmem, vmem],
+        out_specs=(vmem, vmem),
+        compiler_params=pltpu.CompilerParams(vmem_limit_bytes=4 << 20),
+    )(attended, embed_grad)
     return attended[None], embed_grad
 
 

time: 45.6 us -> 42.4 us (0.930)
  local copies, waits for them, and re-layouts: 3.24 us -> 0 us
    unnamed x2 -> x0, local copies, waits for them, and re-layouts: 3.24 us -> none
    pallas_call x1 -> x2, Pallas kernels: 41.5 us -> 41.6 us  [the longest x1 40.8 us: fast_device(): pl.pallas_call(functools.partial(fused, groups, seq), out_shape=(pltpu.VM...]
where the time goes in v2:
time: 42.4 us; the launch traced here: 42.2 us
  Pallas kernels  41.6 us (98%)
  between operations  0.64 us (2%)
    pallas_call x1, Pallas kernels, fast_device(): pl.pallas_call(functools.partial(fused, groups, seq), out_shape=(pltpu.VM...  40.8 us

profile of v2, /device:TPU:1, one launch (start us, length us, event | category | flops | bytes accessed | tf_op | source)
XLA Modules:
  0.0 42.2 jit_solution(461571378448155899)
XLA Ops:
  0.6 40.8 %shard_map.95 = (bf16[32,1024]{1,0:T(8,128)(2,1)S(1)}, bf16[64,1536]{1,0:T(8,128)(2,1)S(1)}) custom-call(bf16[64,512]{1,0:T(8,128)(2,1)} %bitcast.12, bf16[432,512]{1,0:T(8,128)(2,1)} %bitcast.11, f32[1,16]{1,0:T(1,128)} %bitcast.15, s32[1,32]{1,0:T(1,128)} %bitcast.16, bf16[64,3072]{1,0:T(8,128)(2,1)} %embed_hbm.1, f32[1,3072]{1,0:T(1,128)} %bitcast.14, ...), custom_call_target="tpu_custom_call" | custom-call | tf_op jit(solution)/shard_map/pallas_call | solution.py:598
  41.4 0.8 %shard_map.96 = (bf16[32,1024]{1,0:T(8,128)(2,1)}, f32[64,1536]{1,0:T(8,128)}) custom-call(bf16[32,1024]{1,0:T(8,128)(2,1)S(1)} %get-tuple-element.6.att_in, bf16[64,1536]{1,0:T(8,128)(2,1)S(1)} %get-tuple-element.7.grad_in), custom_call_target="tpu_custom_call" | custom-call | tf_op jit(solution)/shard_map/pallas_call | solution.py:647
